TPU v7x, 32 devices: a whole 2x2x4 slice. The times are simulated.
32 devices in a mesh: seq: 16 (over z, y, x), par: 2 (over core).
Axes of the slice: x: 2, y: 2, z: 4, core: 2. Of those that a mesh axis runs over, the one named last changes fastest.
Arguments:
- states: float32 [4096, 128], P('seq'), may hold values from -6 to 6
- cotangent: float32 [4096, 128], P('seq'), may hold values from -6 to 6
- obs_count: int32 [32], P('seq'), may hold values from 16 to 128
- step_index: int32 [2, 4096], P(None, 'seq'), may hold values from 0 to 15
- step_table: float32 [16], replicated, may hold values from 0.05 to 0.25
- w_in: bfloat16 [128, 2048], P(None, 'par'), may hold values from -0.5 to 0.5
- b_hid: bfloat16 [2048], P('par'), may hold values from -3 to 3
- w_out: bfloat16 [128, 2048], P(None, 'par'), may hold values from -0.125 to 0.125
- b_out: float32 [128], replicated, may hold values from -3 to 3
Outputs:
- state_grad: float32 [4096, 128], P('seq')
- grad_in: float32 [128, 2048], P('seq', 'par')
- grad_out: float32 [128, 2048], P('seq', 'par')
All inputs are finite; a program needn't handle non-finite values.
Results may differ from a plain program's by a relative error of at most 0.0055.
Values may be sent and summed in bfloat16 or wider, within the bound.
A program may use at most 64 MiB of HBM per device.

v0:
```python
import jax
import jax.numpy as jnp
from jax import lax
from jax.sharding import PartitionSpec as P

COEF_A = [
    [],
    [1.0 / 5],
    [3.0 / 40, 9.0 / 40],
    [44.0 / 45, -56.0 / 15, 32.0 / 9],
    [19372.0 / 6561, -25360.0 / 2187, 64448.0 / 6561, -212.0 / 729],
    [9017.0 / 3168, -355.0 / 33, 46732.0 / 5247, 49.0 / 176, -5103.0 / 18656],
]
COEF_B = [35.0 / 384, 0.0, 500.0 / 1113, 125.0 / 192, -2187.0 / 6784, 11.0 / 84]


def unchanged(value):
    return value


def field(state, w_in, b_hid, w_out, b_out, forward_sum):
    state_b = state.astype(jnp.bfloat16)
    hidden = jnp.tanh(
        jnp.dot(state_b, w_in, preferred_element_type=jnp.float32) + b_hid.astype(jnp.float32)
    )
    hidden_b = hidden.astype(jnp.bfloat16)
    partial_out = jnp.einsum("rh,lh->rl", hidden_b, w_out, preferred_element_type=jnp.float32)
    return (forward_sum(partial_out) + b_out, state_b, hidden, hidden_b)


def sweep(states, initial, sizes_list, w_in, b_hid, w_out, b_out, forward_sum, backward_sum):
    value = states
    records = []
    for size_now in sizes_list:
        slopes = []
        saved = []
        for current in range(6):
            if current == 0:
                probe = value
            else:
                combo = COEF_A[current][0] * slopes[0]
                for previous in range(1, current):
                    combo = combo + COEF_A[current][previous] * slopes[previous]
                probe = value + size_now * combo
            slope, state_b, hidden, hidden_b = field(probe, w_in, b_hid, w_out, b_out, forward_sum)
            slopes.append(slope)
            saved.append((state_b, hidden, hidden_b))
        combo = COEF_B[0] * slopes[0]
        for current in range(2, 6):
            combo = combo + COEF_B[current] * slopes[current]
        value = value + size_now * combo
        records.append((size_now, saved))
    back = initial
    grad_in = jnp.zeros(w_in.shape, jnp.float32)
    grad_out = jnp.zeros(w_out.shape, jnp.float32)
    for size_now, saved in reversed(records):
        adjoints = [None] * 6
        total = back
        for current in reversed(range(6)):
            combo = COEF_B[current] * back
            for later in range(current + 1, 6):
                combo = combo + COEF_A[later][current] * adjoints[later]
            grad_b = (size_now * combo).astype(jnp.bfloat16)
            state_b, hidden, hidden_b = saved[current]
            inner = jnp.dot(grad_b, w_out, preferred_element_type=jnp.float32) * (
                1.0 - hidden * hidden
            )
            inner_b = inner.astype(jnp.bfloat16)
            partial_back = jnp.einsum(
                "rh,lh->rl", inner_b, w_in, preferred_element_type=jnp.float32
            )
            adjoints[current] = backward_sum(partial_back)
            total = total + adjoints[current]
            grad_in = grad_in + jnp.einsum(
                "rl,rh->lh", state_b, inner_b, preferred_element_type=jnp.float32
            )
            grad_out = grad_out + jnp.einsum(
                "rl,rh->lh", grad_b, hidden_b, preferred_element_type=jnp.float32
            )
        back = total
    return (back, grad_in, grad_out)


def per_device(states, cotangent, obs_count, step_index, step_table, w_in, b_hid, w_out, b_out):
    rows = states.shape[0]
    local_seqs = obs_count.shape[0]
    slot_count = rows // local_seqs
    live = (jnp.arange(slot_count, dtype=jnp.int32)[None, :] < obs_count[:, None]).reshape(rows)
    initial = cotangent * live[:, None].astype(jnp.float32)
    table_ids = jnp.arange(step_table.shape[0], dtype=jnp.int32)

    def lookup(indices):
        picked = jnp.where(indices[:, None] == table_ids[None, :], step_table[None, :], 0.0)
        return jnp.sum(picked, axis=1)[:, None]

    first_size = lookup(step_index[0])
    second_size = lookup(step_index[1])
    whole_in, whole_out, whole_bias = (
        lax.all_gather(w_in, "par", axis=1, tiled=True),
        lax.all_gather(w_out, "par", axis=1, tiled=True),
        lax.all_gather(b_hid[None, :], "par", axis=1, tiled=True),
    )
    half = rows // lax.axis_size("par")
    start = lax.axis_index("par") * half

    def my_half(array):
        return lax.dynamic_slice_in_dim(array, start, half, 0)

    back, grad_in, grad_out = sweep(
        my_half(states),
        my_half(initial),
        (my_half(first_size), my_half(second_size)),
        whole_in,
        whole_bias[0],
        whole_out,
        b_out,
        unchanged,
        unchanged,
    )
    back = lax.all_gather(back, "par", axis=0, tiled=True)
    grad_in, grad_out = (
        lax.psum_scatter(grad_in, "par", scatter_dimension=1, tiled=True),
        lax.psum_scatter(grad_out, "par", scatter_dimension=1, tiled=True),
    )
    grad_in, grad_out = (
        lax.psum_scatter(grad_in, "seq", scatter_dimension=0, tiled=True),
        lax.psum_scatter(grad_out, "seq", scatter_dimension=0, tiled=True),
    )
    return (back, grad_in, grad_out)


def solution(mesh):
    return jax.shard_map(
        per_device,
        mesh=mesh,
        in_specs=(
            P("seq", None),
            P("seq", None),
            P("seq"),
            P(None, "seq"),
            P(),
            P(None, "par"),
            P("par"),
            P(None, "par"),
            P(),
        ),
        out_specs=(P("seq", None), P("seq", "par"), P("seq", "par")),
        check_vma=False,
    )
```

profile of v0, /device:TPU:0, one launch (start us, length us, event | category | flops | bytes accessed | tf_op | source)
XLA Modules:
  0.0 234.0 jit_solution(17293496478932762969)
XLA Ops:
  7.2 0.6 copy-done.51
  8.0 0.7 copy-done.50
  8.9 0.7 copy-done.48
  9.5 2.0 all-gather
  11.5 2.5 %all_gather.13 = bf16[128,2048]{1,0:T(8,128)(2,1)S(1)} all-gather(bf16[128,1024]{1,0:T(8,128)(2,1)} %param.14), channel_id=1, replica_groups=mesh['seq'=16,'par'=2] {'par'}, dimensions={1}, use_global_device_ids=true | all-gather | bytes 786432 | tf_op jit(solution)/shard_map/all_gather | solution.py:99
  14.0 2.3 all_gather.12
  16.6 0.4 copy-done.47
  23.1 0.3 add_convert_fusion.2
  24.1 0.3 add_convert_fusion.1
  25.0 0.3 add_convert_fusion
  26.0 0.3 fusion.32
  27.2 0.3 fusion.12
  27.6 0.4 fusion.33
  28.6 0.3 convolution_add_fusion.10
  28.9 0.5 copy-done.16
  30.0 0.3 convolution_add_fusion.9
  30.4 0.5 copy-done.8
  31.5 0.3 convolution_add_fusion.8
  31.8 0.5 copy-done
  32.9 0.3 convolution_add_fusion.7
  33.2 0.5 copy-done.2
  34.3 0.3 convolution_add_fusion.6
  34.6 0.5 copy-done.10
  35.1 0.3 convolution_add_fusion.35
  35.4 0.3 fusion.18
  35.8 0.4 convolution_add_fusion.5
  36.8 0.3 convolution_add_fusion.4
  37.1 0.5 copy-done.12
  38.2 0.5 convolution_add_fusion.3
  39.6 0.3 convolution_add_fusion.2
  39.9 0.5 copy-done.6
  41.0 0.3 convolution_add_fusion.1
  41.4 0.4 copy-done.14
  41.8 0.9 multiply_convert_fusion
  42.8 0.6 copy-done.24
  43.4 1.3 convolution_add_fusion
  44.8 1.1 fusion.63
  46.0 0.3 convolution_add_fusion.21
  46.3 0.7 copy-done.9
  47.0 0.3 convolution_add_fusion.20
  47.3 0.7 copy-done.1
  48.0 0.3 convolution_add_fusion.19
  48.4 0.7 copy-done.3
  49.1 0.3 convolution_add_fusion.18
  49.4 0.4 copy-done.25
  50.1 0.7 copy-done.11
  50.9 0.3 convolution_add_fusion.17
  51.2 0.4 copy-done.32
  52.0 0.7 copy-done.13
  52.7 0.3 convolution_add_fusion.15
  53.0 0.8 copy-done.5
  53.9 0.3 convolution_add_fusion.14
  54.2 0.7 copy-done.7
  54.9 0.3 convolution_add_fusion.13
  55.2 0.7 copy-done.15
  56.0 0.3 convolution_add_fusion.12
  56.3 1.3 convolution_add_fusion.11
  57.7 0.7 reduce-scatter.11.cloned.1.call-update
  58.4 10.3 %reduce-scatter.5.cloned.1.call-done = f32[128,1024]{1,0:T(8,128)} async-done(((f32[128,2048]{1,0:T(8,128)}), f32[128,1024]{1,0:T(8,128)}) %reduce-scatter.5.cloned.1.call-update) | async-done | bytes 524304 | tf_op jit(solution)/shard_map/reduce_scatter | solution.py:122
  68.7 0.8 copy-done.21
  69.9 1.9 all_gather.15
  71.8 78.4 %reduce-scatter.11.cloned.1.call-done = f32[8,1024]{1,0:T(8,128)} async-done(((f32[128,1024]{1,0:T(8,128)}), f32[8,1024]{1,0:T(8,128)}) %reduce-scatter.11.cloned.1.call-update) | async-done | bytes 32784 | tf_op jit(solution)/shard_map/reduce_scatter | solution.py:127
  150.2 76.6 %reduce-scatter.7.cloned.1.call-done = f32[8,1024]{1,0:T(8,128)} async-done(((f32[128,1024]{1,0:T(8,128)}), f32[8,1024]{1,0:T(8,128)}) %reduce-scatter.7.cloned.1.call-update) | async-done | bytes 32784 | tf_op jit(solution)/shard_map/reduce_scatter | solution.py:126
  226.8 0.7 copy.13
  (136 shorter events, 16.2 us)
Async XLA Ops:
  7.2 50.5 %reduce-scatter.9.cloned.1.call-start = ((), (), s32[]{:S(2)}) async-start(), calls=%async_computation.6 | async-start | bytes 1572864 | tf_op jit(solution)/shard_map/reduce_scatter | solution.py:123
  7.2 0.7 copy-start.51
  7.2 0.7 copy-start.49
  8.0 0.7 copy-start.50
  8.9 0.7 copy-start.48
  11.5 2.5 %copy-start.45 = (bf16[128,1024]{1,0:T(8,128)(2,1)S(1)}, bf16[128,1024]{1,0:T(8,128)(2,1)}, u32[]{:S(2)}) copy-start(bf16[128,1024]{1,0:T(8,128)(2,1)} %param.16) | copy-start | bytes 786436
  14.0 2.3 copy-start.19
  16.3 0.7 copy-start.47
  17.3 0.6 copy-start.39
  18.2 0.6 copy-start.43
  19.1 0.6 copy-start.27
  20.1 0.6 copy-start.29
  21.0 0.6 copy-start.31
  22.5 0.6 copy-start.41
  23.5 0.6 copy-start.33
  24.4 0.6 copy-start.35
  25.3 0.6 copy-start.37
  26.3 0.6 copy-start.26
  26.3 0.9 copy-start.18
  28.6 0.8 copy-start.16
  30.0 0.8 copy-start.8
  31.4 0.8 copy-start
  32.9 0.8 copy-start.2
  34.3 0.8 copy-start.10
  36.8 0.8 copy-start.12
  38.2 0.8 copy-start.4
  39.3 2.1 copy-start.20
  39.6 0.8 copy-start.6
  40.7 0.7 copy-start.22
  41.0 0.8 copy-start.14
  42.8 0.6 copy-start.24
  44.7 24.0 %reduce-scatter.5.cloned.1.call-start = ((), (), s32[]{:S(2)}) async-start(), calls=%async_computation.4 | async-start | bytes 1572864 | tf_op jit(solution)/shard_map/reduce_scatter | solution.py:122
  44.8 1.2 copy-start.17
  44.8 1.2 copy-start.38
  46.0 1.0 copy-start.9
  46.0 1.0 copy-start.36
  47.0 1.0 copy-start.1
  47.0 1.0 copy-start.34
  48.0 1.0 copy-start.3
  48.0 1.0 copy-start.42
  49.1 0.8 copy-start.25
  49.8 1.0 copy-start.11
  50.9 0.8 copy-start.32
  51.6 1.0 copy-start.13
  51.7 1.0 copy-start.30
  52.7 1.2 copy-start.5
  52.7 1.2 copy-start.28
  53.9 1.0 copy-start.7
  53.9 1.0 copy-start.44
  54.9 1.1 copy-start.15
  54.9 1.1 copy-start.40
  57.6 92.6 %reduce-scatter.11.cloned.1.call-start = ((), (), s32[]{:S(2)}) async-start(), calls=%async_computation.7 | async-start | bytes 557056 | tf_op jit(solution)/shard_map/reduce_scatter | solution.py:127
  58.4 168.4 %reduce-scatter.7.cloned.1.call-start = ((), (), s32[]{:S(2)}) async-start(), calls=%async_computation.5 | async-start | bytes 557056 | tf_op jit(solution)/shard_map/reduce_scatter | solution.py:126
  68.7 0.8 copy-start.21
  68.7 0.9 copy-start.23
  68.7 0.9 copy-start.46
Sparse Core Ops, SparseCore 0:
  44.9 10.9 reduce-scatter.8
  58.1 10.5 reduce-scatter.4
  71.5 78.6 reduce-scatter.10
  152.9 73.8 reduce-scatter.6
where the time goes:
time: 235 us; the launch traced here: 234 us
  waiting for transfers between devices  166 us (71%)
  matrix products  25.7 us (11%)
  local copies, waits for them, and re-layouts  18.7 us (8%)
  between operations  14.5 us (6%)
  blocking collectives  8.69 us (4%)
    reduce_scatter x1, waiting for transfers between devices, per_device(): lax.psum_scatter(grad_out, 'seq', scatter_dimension=0, tiled=True)  78.4 us
    reduce_scatter x1, waiting for transfers between devices, per_device(): lax.psum_scatter(grad_in, 'seq', scatter_dimension=0, tiled=True)  76.6 us
    unnamed x105, local copies, waits for them, and re-layouts  18.6 us
    reduce_scatter x1, waiting for transfers between devices, per_device(): lax.psum_scatter(grad_in, 'par', scatter_dimension=1, tiled=True)  10.3 us
    dot_general x12, matrix products, sweep(): jnp.einsum('rl,rh->lh', state_b, inner_b, preferred_element_type=jnp.floa...  5.65 us
    dot_general x12, matrix products, sweep(): jnp.einsum('rl,rh->lh', grad_b, hidden_b, preferred_element_type=jnp.floa...  5.21 us
  transfers between devices with their start and end apart: 4, of which 3 were waited for; matrix products, arithmetic and copies ran while one was open for 3% of the time, Pallas kernels for 0%

commit v1 on v0

v1 whole, which is shorter than its diff:
```python
import functools

import jax
import jax.numpy as jnp
from jax import lax
from jax.experimental import pallas as pl
from jax.experimental.pallas import tpu as pltpu
from jax.sharding import PartitionSpec as P

COEF_A = [
    [],
    [1.0 / 5],
    [3.0 / 40, 9.0 / 40],
    [44.0 / 45, -56.0 / 15, 32.0 / 9],
    [19372.0 / 6561, -25360.0 / 2187, 64448.0 / 6561, -212.0 / 729],
    [9017.0 / 3168, -355.0 / 33, 46732.0 / 5247, 49.0 / 176, -5103.0 / 18656],
]
COEF_B = [35.0 / 384, 0.0, 500.0 / 1113, 125.0 / 192, -2187.0 / 6784, 11.0 / 84]
STAGES = 6
STEPS = 2
MESH = pl.DeviceIdType.MESH
F32 = jnp.float32
BF16 = jnp.bfloat16
FIELD_COLS = 512
GRAD_COLS = 512


def dot(a, b):
    return jnp.dot(a, b, preferred_element_type=F32)


def weighted(coefs, values):
    total = None
    for coef, value in zip(coefs, values):
        if coef != 0.0:
            term = coef * value
            total = term if total is None else total + term
    return total


def divisor(total, want):
    size = min(total, want)
    while total % size:
        size -= 128
    return size


class Plan:
    def __init__(self, n_seq, n_par, rows, lat, hid_local):
        self.n_seq, self.n_par = n_seq, n_par
        self.half = rows // n_par
        self.lat, self.hid_local = lat, hid_local
        self.field_cols = divisor(hid_local, FIELD_COLS)
        self.cols = divisor(hid_local, GRAD_COLS)
        self.per_grad = hid_local // self.cols
        self.chunks = 2 * self.per_grad
        self.bits = n_seq.bit_length() - 1
        self.piece = lat // n_seq
        self.scatter = n_seq > 1 and n_seq == 1 << self.bits and lat % (8 * n_seq) == 0
        low = tuple(range(self.bits // 2))
        high = tuple(range(self.bits // 2, self.bits))
        self.orders = []
        if self.scatter:
            for chunk in range(self.chunks):
                order = (high, low) if chunk == 0 else (low, high)
                self.orders.append([group for group in order if group])

    def masks(self, group):
        found = []
        for code in range(1, 1 << len(group)):
            found.append(tuple(bit for place, bit in enumerate(group) if code >> place & 1))
        return found


def kernel(
    plan,
    states,
    cotangent,
    obs_count,
    step_index,
    step_table,
    w_in,
    b_hid,
    w_out,
    b_out,
    *rest,
):
    out_back, out_in, out_out = rest[:3]
    (
        win, wout, bias, win_t, wout_t, sizes, hid, hid_b, inner_b, vb_t, gb_t,
        give, take, own,
        weight_sems, give_sems, back_sems,
    ) = rest[3:20]
    stage_refs = rest[20:]
    n_par, half, hl, cols = plan.n_par, plan.half, plan.hid_local, plan.cols
    par = lax.axis_index("par")
    seq = lax.axis_index("seq")
    bit_of = [(seq // (1 << b)) % 2 for b in range(plan.bits)]

    def across(mask):
        partner = seq
        for b in mask:
            partner = partner + (1 - 2 * bit_of[b]) * (1 << b)
        return partner

    peers = [lax.rem(par + k, n_par) for k in range(n_par)]
    barrier = pltpu.get_barrier_semaphore()
    greeted = 0
    for k in range(1, n_par):
        pl.semaphore_signal(barrier, inc=1, device_id={"par": peers[k]}, device_id_type=MESH)
        greeted += 1
    if plan.scatter:
        for group in plan.orders[0]:
            for mask in plan.masks(group):
                pl.semaphore_signal(
                    barrier, inc=1, device_id={"seq": across(mask)}, device_id_type=MESH
                )
                greeted += 1

    start = par * half
    rows_here = pl.ds(pl.multiple_of(start, 128), half)
    index = step_index[:, rows_here]
    size_rows = jnp.zeros(index.shape, F32)
    for entry in range(step_table.shape[0]):
        size_rows = jnp.where(index == entry, step_table[entry], size_rows)
    for step in range(STEPS):
        spread = jnp.broadcast_to(size_rows[step : step + 1], (plan.lat, half))
        sizes[step] = spread.T
    local_seqs = obs_count.shape[0]
    slot = states.shape[0] // local_seqs
    row = start + lax.broadcasted_iota(jnp.int32, (half, plan.lat), 0)
    live = jnp.zeros((half, plan.lat), F32)
    for one in range(local_seqs):
        first = one * slot
        inside = (row >= first) & (row < first + obs_count[one])
        live = jnp.where(inside, 1.0, live)

    def copies_of_weights():
        made = []
        for k in range(1, n_par):
            for which, (src, dst) in enumerate(
                ((w_in, win), (w_out, wout), (b_hid, bias))
            ):
                made.append(
                    pltpu.make_async_remote_copy(
                        src_ref=src,
                        dst_ref=dst.at[n_par - k - 1],
                        send_sem=weight_sems.at[0, k - 1, which],
                        recv_sem=weight_sems.at[1, n_par - k - 1, which],
                        device_id={"par": peers[k]},
                        device_id_type=MESH,
                    )
                )
        return made

    def transposed(k, in_ref, out_ref):
        win_t[k * hl : (k + 1) * hl, :] = in_ref[...].T
        wout_t[k * hl : (k + 1) * hl, :] = out_ref[...].T

    pl.semaphore_wait(barrier, greeted)
    weights = copies_of_weights()
    for copy in weights:
        copy.start()
    transposed(0, w_in, w_out)
    for copy in weights:
        copy.wait()
    for k in range(1, n_par):
        transposed(k, win.at[k - 1], wout.at[k - 1])

    def pieces():
        for k in range(n_par):
            for c in range(0, hl, plan.field_cols):
                here = slice(c, c + plan.field_cols)
                there = slice(k * hl + c, k * hl + c + plan.field_cols)
                yield k, here, there

    def w_in_at(k, here):
        return w_in[:, here] if k == 0 else win[k - 1, :, here]

    def w_out_at(k, here):
        return w_out[:, here] if k == 0 else wout[k - 1, :, here]

    def bias_at(k, here):
        return b_hid[:, here] if k == 0 else bias[k - 1, :, here]

    def forward(step, value):
        size = sizes[step]
        slopes = []
        for current in range(STAGES):
            at = step * STAGES + current
            probe = value
            if current:
                probe = value + size * weighted(COEF_A[current], slopes)
            state_b = probe.astype(BF16)
            vb_t[at] = state_b.T
            slope = jnp.broadcast_to(b_out[...], (half, plan.lat))
            for k, here, there in pieces():
                hidden = jnp.tanh(dot(state_b, w_in_at(k, here)) + bias_at(k, here))
                hidden_b = hidden.astype(BF16)
                hid[at, :, there] = 1.0 - hidden * hidden
                hid_b[at, :, there] = hidden_b
                slope = slope + dot(hidden_b, wout_t[there, :])
            slopes.append(slope)
        return value + size * weighted(COEF_B, slopes)

    lax.fori_loop(0, STEPS, forward, states[rows_here, :])

    def backward(turn, back):
        step = STEPS - 1 - turn
        size = sizes[step]
        adjoints = [None] * STAGES
        total = back
        for current in reversed(range(STAGES)):
            at = step * STAGES + current
            coefs = [COEF_B[current]] + [
                COEF_A[later][current] for later in range(current + 1, STAGES)
            ]
            grad_b = (size * weighted(coefs, [back] + adjoints[current + 1 :])).astype(BF16)
            gb_t[at] = grad_b.T
            adjoint = None
            for k, here, there in pieces():
                inner = (dot(grad_b, w_out_at(k, here)) * hid[at, :, there]).astype(BF16)
                inner_b[at, :, there] = inner
                part = dot(inner, win_t[there, :])
                adjoint = part if adjoint is None else adjoint + part
            adjoints[current] = adjoint
            total = total + adjoint
        return total

    initial = cotangent[rows_here, :] * live
    out_back[rows_here, :] = lax.fori_loop(0, STEPS, backward, initial)

    def gradient(k, chunk):
        left, right = (vb_t, inner_b) if chunk < plan.per_grad else (gb_t, hid_b)
        begin = k * hl + (chunk % plan.per_grad) * cols
        lhs = jnp.concatenate([left[at] for at in range(STEPS * STAGES)], axis=1)
        rhs = right[:, :, begin : begin + cols].reshape(STEPS * STAGES * half, cols)
        return dot(lhs, rhs)

    waiting = []
    given = {}
    for k in range(1, n_par):
        for chunk in range(plan.chunks):
            give[k - 1, chunk] = gradient(k, chunk).astype(BF16)
            copy = pltpu.make_async_remote_copy(
                src_ref=give.at[k - 1, chunk],
                dst_ref=take.at[n_par - k - 1, chunk],
                send_sem=give_sems.at[0, k - 1, chunk],
                recv_sem=give_sems.at[1, n_par - k - 1, chunk],
                device_id={"par": peers[k]},
                device_id_type=MESH,
            )
            copy.start()
            given[n_par - k - 1, chunk] = copy
            waiting.append(copy)
    back_copies = []
    for k in range(1, n_par):
        copy = pltpu.make_async_remote_copy(
            src_ref=out_back.at[rows_here, :],
            dst_ref=out_back.at[rows_here, :],
            send_sem=back_sems.at[0, k - 1],
            recv_sem=back_sems.at[1, n_par - k - 1],
            device_id={"par": peers[k]},
            device_id_type=MESH,
        )
        copy.start()
        back_copies.append(copy)

    def target(chunk):
        ref = out_in if chunk < plan.per_grad else out_out
        begin = (chunk % plan.per_grad) * cols
        return ref, slice(begin, begin + cols)

    flights = {}

    def launch(chunk, stage):
        send, land, sems = stage_refs[3 * stage : 3 * stage + 3]
        group = plan.orders[chunk][stage]
        left = [b for b in reversed(range(plan.bits)) if b not in sum(plan.orders[chunk][:stage], ())]
        for place, mask in enumerate(plan.masks(group)):
            where = tuple(
                (1 - bit_of[b] if b in mask else bit_of[b]) if b in group else slice(None)
                for b in left
            )
            copy = pltpu.make_async_remote_copy(
                src_ref=send.at[(chunk,) + where],
                dst_ref=land.at[chunk, place],
                send_sem=sems.at[0, chunk, place],
                recv_sem=sems.at[1, chunk, place],
                device_id={"seq": across(mask)},
                device_id_type=MESH,
            )
            copy.start()
            flights.setdefault((chunk, stage), []).append(copy)
            waiting.append(copy)

    for chunk in range(plan.chunks):
        total = gradient(0, chunk)
        for k in range(1, n_par):
            given[k - 1, chunk].wait_recv()
            total = total + take[k - 1, chunk].astype(F32)
        if plan.scatter:
            total = total.reshape((2,) * plan.bits + (plan.piece, cols))
            own[chunk] = total
            stage_refs[0][chunk] = total.astype(BF16)
            launch(chunk, 0)
        else:
            ref, columns = target(chunk)
            ref[:, columns] = total

    if plan.scatter:
        kept = {}
        levels = len(plan.orders[0])
        for stage in range(levels):
            land = stage_refs[3 * stage + 1]
            for chunk in range(plan.chunks):
                group = plan.orders[chunk][stage]
                left = [b for b in reversed(range(plan.bits)) if b not in sum(plan.orders[chunk][:stage], ())]
                where = tuple(bit_of[b] if b in group else slice(None) for b in left)
                total = own[(chunk,) + where] if stage == 0 else kept[chunk].at_own(where)
                for place, copy in enumerate(flights[chunk, stage]):
                    copy.wait_recv()
                    total = total + land[chunk, place].astype(F32)
                if stage == levels - 1:
                    ref, columns = target(chunk)
                    ref[:, columns] = total
                else:
                    own_next = stage_refs[-1]
                    own_next[chunk] = total
                    stage_refs[3 * (stage + 1)][chunk] = total.astype(BF16)
                    kept[chunk] = Kept(own_next, chunk)
                    launch(chunk, stage + 1)

    for copy in waiting:
        copy.wait_send()
    for chunk in given.values() if not plan.scatter else ():
        pass
    for copy in back_copies:
        copy.wait()


class Kept:
    def __init__(self, ref, chunk):
        self.ref, self.chunk = ref, chunk

    def at_own(self, where):
        return self.ref[(self.chunk,) + where]


def per_device(
    states, cotangent, obs_count, step_index, step_table, w_in, b_hid, w_out, b_out
):
    n_seq, n_par = lax.axis_size("seq"), lax.axis_size("par")
    rows, lat = states.shape
    hl = w_in.shape[1]
    plan = Plan(n_seq, n_par, rows, lat, hl)
    half, hidden, sections = plan.half, hl * n_par, STEPS * STAGES
    others = max(n_par - 1, 1)
    vmem = pltpu.VMEM
    dma = pltpu.SemaphoreType.DMA
    scratch = [
        vmem((others, lat, hl), BF16),
        vmem((others, lat, hl), BF16),
        vmem((others, 1, hl), F32),
        vmem((hidden, lat), BF16),
        vmem((hidden, lat), BF16),
        vmem((STEPS, half, lat), F32),
        vmem((sections, half, hidden), F32),
        vmem((sections, half, hidden), BF16),
        vmem((sections, half, hidden), BF16),
        vmem((sections, lat, half), BF16),
        vmem((sections, lat, half), BF16),
        vmem((others, plan.chunks, lat, plan.cols), BF16),
        vmem((others, plan.chunks, lat, plan.cols), BF16),
        vmem(
            (plan.chunks,) + ((2,) * plan.bits + (plan.piece, plan.cols) if plan.scatter else (8, 128)),
            F32,
        ),
        dma((2, others, 3)),
        dma((2, others, plan.chunks)),
        dma((2, others)),
    ]
    grad_rows = plan.piece if plan.scatter else lat
    if plan.scatter:
        left = plan.bits
        for group_size in [len(group) for group in plan.orders[0]]:
            tail = (plan.piece, plan.cols)
            masks = (1 << group_size) - 1
            scratch.append(vmem((plan.chunks,) + (2,) * left + tail, BF16))
            left -= group_size
            scratch.append(vmem((plan.chunks, masks) + (2,) * left + tail, BF16))
            scratch.append(dma((2, plan.chunks, masks)))
        middle = plan.bits - len(plan.orders[0][0])
        scratch.append(vmem((plan.chunks,) + (2,) * middle + (plan.piece, plan.cols), F32))
    in_vmem = pl.BlockSpec(memory_space=pltpu.VMEM)
    in_smem = pl.BlockSpec(memory_space=pltpu.SMEM)
    back, grad_in, grad_out = pl.pallas_call(
        functools.partial(kernel, plan),
        name="adjoint",
        out_shape=(
            jax.ShapeDtypeStruct((rows, lat), F32),
            jax.ShapeDtypeStruct((grad_rows, hl), F32),
            jax.ShapeDtypeStruct((grad_rows, hl), F32),
        ),
        in_specs=[in_vmem, in_vmem, in_smem, in_vmem, in_smem] + [in_vmem] * 4,
        out_specs=(in_vmem,) * 3,
        scratch_shapes=scratch,
        compiler_params=pltpu.CompilerParams(
            collective_id=0,
            has_side_effects=True,
            vmem_limit_bytes=60 * 1024 * 1024,
        ),
    )(
        states,
        cotangent,
        obs_count,
        step_index,
        step_table,
        w_in,
        b_hid.astype(F32)[None, :],
        w_out,
        b_out[None, :],
    )
    if not plan.scatter:
        grad_in, grad_out = (
            lax.psum_scatter(grad, "seq", scatter_dimension=0, tiled=True)
            for grad in (grad_in, grad_out)
        )
    return (back, grad_in, grad_out)


def solution(mesh):
    return jax.shard_map(
        per_device,
        mesh=mesh,
        in_specs=(
            P("seq", None),
            P("seq", None),
            P("seq"),
            P(None, "seq"),
            P(),
            P(None, "par"),
            P("par"),
            P(None, "par"),
            P(),
        ),
        out_specs=(P("seq", None), P("seq", "par"), P("seq", "par")),
        check_vma=False,
    )
```

time: 235 us -> 46.2 us (0.20)
  waiting for transfers between devices: 166 us -> 0 us
  Pallas kernels: 0 us -> 41 us
  matrix products: 25.7 us -> 0 us
  local copies, waits for them, and re-layouts: 18.7 us -> 2.96 us
  between operations: 14.5 us -> 0.65 us
  blocking collectives: 8.69 us -> 0 us
    reduce_scatter x4 -> x0, waiting for transfers between devices: 165 us -> none  [the longest x1 78.4 us: per_device(): lax.psum_scatter(grad_out, 'seq', scatter_dimension=0, tiled=True)]
    pallas_call x0 -> x1, Pallas kernels: none -> 41 us  [per_device(): pl.pallas_call(functools.partial(kernel, plan), name='adjoint', out_shape...]
    dot_general x71 -> x0, matrix products: 25.7 us -> none  [the longest x12 5.65 us: sweep(): jnp.einsum('rl,rh->lh', state_b, inner_b, preferred_element_type=jnp.floa...]
    unnamed x105 -> x7, local copies, waits for them, and re-layouts: 18.6 us -> 2.96 us
    all_gather x4 -> x0, blocking collectives: 8.69 us -> none  [the longest x1 2.51 us: per_device(): lax.all_gather(w_in, 'par', axis=1, tiled=True)]
  transfers between devices with their start and end apart: 4 -> 0, of which waited for: 3 -> 0; matrix products, arithmetic and copies ran while one was open for 3% -> 0% of each run, Pallas kernels for 0% -> 0%
where the time goes in v1:
time: 46.2 us; the launch traced here: 45.9 us
  Pallas kernels  41 us (89%)
  local copies, waits for them, and re-layouts  2.96 us (6%)
  other arithmetic  1.28 us (3%)
  between operations  0.65 us (1%)
    pallas_call x1, Pallas kernels, per_device(): pl.pallas_call(functools.partial(kernel, plan), name='adjoint', out_shape...  41 us
    unnamed x7, local copies, waits for them, and re-layouts  2.96 us
    broadcast_in_dim x1, other arithmetic, per_device(): b_hid.astype(F32)[None, :]  1.28 us

profile of v1, /device:TPU:0, one launch (start us, length us, event | category | flops | bytes accessed | tf_op | source)
XLA Modules:
  0.0 45.9 jit_solution(621314029858023490)
XLA Ops:
  0.6 1.3 %broadcast_in_dim.11 = f32[1024]{0:T(1024)} convert(bf16[1024]{0:T(1024)(128)(2,1)} %param.15) | non-fusion elementwise | flops 1024 | bytes 6144 | tf_op jit(solution)/shard_map/broadcast_in_dim | solution.py:420
  1.9 41.0 %adjoint.1 = (f32[256,128]{1,0:T(8,128)}, f32[8,1024]{1,0:T(8,128)}, f32[8,1024]{1,0:T(8,128)}) custom-call(f32[256,128]{1,0:T(8,128)} %states.1, f32[256,128]{1,0:T(8,128)} %cotangent.1, s32[2]{0:T(128)} %obs_count.1, s32[2,256]{1,0:T(2,128)} %step_index.1, f32[16]{0:T(128)} %step_table.1, bf16[128,1024]{1,0:T(8,128)(2,1)} %w_in.1, f32[1,1024]{1,0:T(1,128)} %bitcast.2, ...), custom_call_target="tpu_custom_call" | custom-call | tf_op jit(solution)/shard_map/adjoint/pallas_call | solution.py:397
  43.0 0.0 copy-start.1
  43.0 1.6 %copy.15 = f32[256,128]{1,0:T(8,128)} copy(f32[256,128]{1,0:T(8,128)} %get-tuple-element.6) | data formatting | bytes 262144
  44.5 0.0 copy-done.1
  44.5 0.0 copy-start
  44.5 0.6 %copy.16 = f32[8,1024]{1,0:T(8,128)} copy(f32[8,1024]{1,0:T(8,128)S(1)} %copy-done.1) | data formatting | bytes 65536
  45.2 0.2 copy-done
  45.3 0.6 %copy.17 = f32[8,1024]{1,0:T(8,128)} copy(f32[8,1024]{1,0:T(8,128)S(1)} %copy-done) | data formatting | bytes 65536
Async XLA Ops:
  43.0 1.6 %copy-start.1 = (f32[8,1024]{1,0:T(8,128)S(1)}, f32[8,1024]{1,0:T(8,128)}, u32[]{:S(2)}) copy-start(f32[8,1024]{1,0:T(8,128)} %get-tuple-element.7) | copy-start | bytes 98308
  44.5 0.8 %copy-start = (f32[8,1024]{1,0:T(8,128)S(1)}, f32[8,1024]{1,0:T(8,128)}, u32[]{:S(2)}) copy-start(f32[8,1024]{1,0:T(8,128)} %get-tuple-element.8) | copy-start | bytes 98308

commit v2 on v1

--- a/solution.py
+++ b/solution.py
@@ -45,6 +45,10 @@
     return size
 
 
+def orders_of(chunk, low, high):
+    return (high, low) if chunk == 0 else (low, high)
+
+
 class Plan:
     def __init__(self, n_seq, n_par, rows, lat, hid_local):
         self.n_seq, self.n_par = n_seq, n_par
@@ -60,10 +64,27 @@
         low = tuple(range(self.bits // 2))
         high = tuple(range(self.bits // 2, self.bits))
         self.orders = []
+        self.base = []
+        self.messages = 0
         if self.scatter:
             for chunk in range(self.chunks):
-                order = (high, low) if chunk == 0 else (low, high)
+                order = orders_of(chunk, low, high)
                 self.orders.append([group for group in order if group])
+                self.base.append([])
+                for group in self.orders[-1]:
+                    self.base[-1].append(self.messages)
+                    self.messages += (1 << len(group)) - 1
+
+    def left(self, chunk, stage):
+        gone = sum(self.orders[chunk][:stage], ())
+        return [b for b in reversed(range(self.bits)) if b not in gone]
+
+    def partners(self):
+        found = set()
+        for order in self.orders:
+            for group in order:
+                found.update(self.masks(group))
+        return sorted(found)
 
     def masks(self, group):
         found = []
@@ -74,28 +95,52 @@
 
 def kernel(
     plan,
-    states,
-    cotangent,
-    obs_count,
-    step_index,
-    step_table,
-    w_in,
-    b_hid,
-    w_out,
-    b_out,
+    states_h,
+    cotangent_h,
+    obs_count_h,
+    step_index_h,
+    step_table_h,
+    w_in_h,
+    b_hid_h,
+    w_out_h,
+    b_out_h,
     *rest,
 ):
     out_back, out_in, out_out = rest[:3]
     (
+        states, cotangent, obs_count, step_index, step_table, w_in, b_hid, w_out, b_out,
+        local_sems,
         win, wout, bias, win_t, wout_t, sizes, hid, hid_b, inner_b, vb_t, gb_t,
-        give, take, own,
+        give, take,
         weight_sems, give_sems, back_sems,
-    ) = rest[3:20]
-    stage_refs = rest[20:]
+    ) = rest[3:29]
+    stage_refs = rest[29:]
+    if plan.scatter:
+        seq_sems = stage_refs[0]
+        stage_refs = stage_refs[1:]
     n_par, half, hl, cols = plan.n_par, plan.half, plan.hid_local, plan.cols
     par = lax.axis_index("par")
     seq = lax.axis_index("seq")
     bit_of = [(seq // (1 << b)) % 2 for b in range(plan.bits)]
+    start = par * half
+    rows_here = pl.ds(pl.multiple_of(start, 128), half)
+
+    loads = {}
+    for place, (name, src, dst) in enumerate(
+        (
+            ("w_in", w_in_h, w_in),
+            ("w_out", w_out_h, w_out),
+            ("b_hid", b_hid_h, b_hid),
+            ("step_index", step_index_h, step_index),
+            ("step_table", step_table_h, step_table),
+            ("states", states_h.at[rows_here, :], states),
+            ("b_out", b_out_h, b_out),
+            ("cotangent", cotangent_h.at[rows_here, :], cotangent),
+            ("obs_count", obs_count_h, obs_count),
+        )
+    ):
+        loads[name] = pltpu.make_async_copy(src, dst, local_sems.at[place])
+        loads[name].start()
 
     def across(mask):
         partner = seq
@@ -106,34 +151,19 @@
     peers = [lax.rem(par + k, n_par) for k in range(n_par)]
     barrier = pltpu.get_barrier_semaphore()
     greeted = 0
+    for mask in plan.partners():
+        pl.semaphore_signal(barrier, inc=1, device_id={"seq": across(mask)}, device_id_type=MESH)
+        greeted += 1
     for k in range(1, n_par):
         pl.semaphore_signal(barrier, inc=1, device_id={"par": peers[k]}, device_id_type=MESH)
         greeted += 1
-    if plan.scatter:
-        for group in plan.orders[0]:
-            for mask in plan.masks(group):
-                pl.semaphore_signal(
-                    barrier, inc=1, device_id={"seq": across(mask)}, device_id_type=MESH
-                )
-                greeted += 1
-
-    start = par * half
-    rows_here = pl.ds(pl.multiple_of(start, 128), half)
-    index = step_index[:, rows_here]
-    size_rows = jnp.zeros(index.shape, F32)
-    for entry in range(step_table.shape[0]):
-        size_rows = jnp.where(index == entry, step_table[entry], size_rows)
-    for step in range(STEPS):
-        spread = jnp.broadcast_to(size_rows[step : step + 1], (plan.lat, half))
-        sizes[step] = spread.T
-    local_seqs = obs_count.shape[0]
-    slot = states.shape[0] // local_seqs
-    row = start + lax.broadcasted_iota(jnp.int32, (half, plan.lat), 0)
-    live = jnp.zeros((half, plan.lat), F32)
-    for one in range(local_seqs):
-        first = one * slot
-        inside = (row >= first) & (row < first + obs_count[one])
-        live = jnp.where(inside, 1.0, live)
+
+    def transposed(k, in_ref, out_ref):
+        win_t[k * hl : (k + 1) * hl, :] = in_ref[...].T
+        wout_t[k * hl : (k + 1) * hl, :] = out_ref[...].T
+
+    for name in ("w_in", "w_out", "b_hid"):
+        loads[name].wait()
 
     def copies_of_weights():
         made = []
@@ -153,15 +183,31 @@
                 )
         return made
 
-    def transposed(k, in_ref, out_ref):
-        win_t[k * hl : (k + 1) * hl, :] = in_ref[...].T
-        wout_t[k * hl : (k + 1) * hl, :] = out_ref[...].T
-
-    pl.semaphore_wait(barrier, greeted)
+    if greeted:
+        pl.semaphore_wait(barrier, greeted)
     weights = copies_of_weights()
     for copy in weights:
         copy.start()
     transposed(0, w_in, w_out)
+    for name in ("step_index", "step_table", "states", "b_out", "cotangent", "obs_count"):
+        loads[name].wait()
+
+    index = step_index[:, rows_here]
+    size_rows = jnp.zeros(index.shape, F32)
+    for entry in range(step_table.shape[0]):
+        size_rows = jnp.where(index == entry, step_table[entry], size_rows)
+    for step in range(STEPS):
+        spread = jnp.broadcast_to(size_rows[step : step + 1], (plan.lat, half))
+        sizes[step] = spread.T
+    local_seqs = obs_count.shape[0]
+    slot = states_h.shape[0] // local_seqs
+    row = start + lax.broadcasted_iota(jnp.int32, (half, plan.lat), 0)
+    live = jnp.zeros((half, plan.lat), F32)
+    for one in range(local_seqs):
+        first = one * slot
+        inside = (row >= first) & (row < first + obs_count[one])
+        live = jnp.where(inside, 1.0, live)
+
     for copy in weights:
         copy.wait()
     for k in range(1, n_par):
@@ -196,14 +242,13 @@
             slope = jnp.broadcast_to(b_out[...], (half, plan.lat))
             for k, here, there in pieces():
                 hidden = jnp.tanh(dot(state_b, w_in_at(k, here)) + bias_at(k, here))
-                hidden_b = hidden.astype(BF16)
                 hid[at, :, there] = 1.0 - hidden * hidden
-                hid_b[at, :, there] = hidden_b
-                slope = slope + dot(hidden_b, wout_t[there, :])
+                hid_b[at, :, there] = hidden.astype(BF16)
+            slope = slope + dot(hid_b[at], wout_t[...])
             slopes.append(slope)
         return value + size * weighted(COEF_B, slopes)
 
-    lax.fori_loop(0, STEPS, forward, states[rows_here, :])
+    lax.fori_loop(0, STEPS, forward, states[...])
 
     def backward(turn, back):
         step = STEPS - 1 - turn
@@ -217,17 +262,15 @@
             ]
             grad_b = (size * weighted(coefs, [back] + adjoints[current + 1 :])).astype(BF16)
             gb_t[at] = grad_b.T
-            adjoint = None
             for k, here, there in pieces():
-                inner = (dot(grad_b, w_out_at(k, here)) * hid[at, :, there]).astype(BF16)
-                inner_b[at, :, there] = inner
-                part = dot(inner, win_t[there, :])
-                adjoint = part if adjoint is None else adjoint + part
+                inner = dot(grad_b, w_out_at(k, here)) * hid[at, :, there]
+                inner_b[at, :, there] = inner.astype(BF16)
+            adjoint = dot(inner_b[at], win_t[...])
             adjoints[current] = adjoint
             total = total + adjoint
         return total
 
-    initial = cotangent[rows_here, :] * live
+    initial = cotangent[...] * live
     out_back[rows_here, :] = lax.fori_loop(0, STEPS, backward, initial)
 
     def gradient(k, chunk):
@@ -271,27 +314,38 @@
         begin = (chunk % plan.per_grad) * cols
         return ref, slice(begin, begin + cols)
 
+    refs = {}
+    if plan.scatter:
+        count = 0
+        for chunk in range(plan.chunks):
+            for stage in range(len(plan.orders[chunk])):
+                refs[chunk, stage] = stage_refs[count : count + 3]
+                count += 3
     flights = {}
 
-    def launch(chunk, stage):
-        send, land, sems = stage_refs[3 * stage : 3 * stage + 3]
+    def launch(chunk, stage, total):
+        keep, send, land = refs[chunk, stage]
+        keep[...] = total
+        send[...] = total.astype(BF16)
         group = plan.orders[chunk][stage]
-        left = [b for b in reversed(range(plan.bits)) if b not in sum(plan.orders[chunk][:stage], ())]
+        left = plan.left(chunk, stage)
+        flights[chunk, stage] = []
         for place, mask in enumerate(plan.masks(group)):
             where = tuple(
                 (1 - bit_of[b] if b in mask else bit_of[b]) if b in group else slice(None)
                 for b in left
             )
+            number = plan.base[chunk][stage] + place
             copy = pltpu.make_async_remote_copy(
-                src_ref=send.at[(chunk,) + where],
-                dst_ref=land.at[chunk, place],
-                send_sem=sems.at[0, chunk, place],
-                recv_sem=sems.at[1, chunk, place],
+                src_ref=send.at[where],
+                dst_ref=land.at[place],
+                send_sem=seq_sems.at[0, number],
+                recv_sem=seq_sems.at[1, number],
                 device_id={"seq": across(mask)},
                 device_id_type=MESH,
             )
             copy.start()
-            flights.setdefault((chunk, stage), []).append(copy)
+            flights[chunk, stage].append(copy)
             waiting.append(copy)
 
     for chunk in range(plan.chunks):
@@ -300,51 +354,35 @@
             given[k - 1, chunk].wait_recv()
             total = total + take[k - 1, chunk].astype(F32)
         if plan.scatter:
-            total = total.reshape((2,) * plan.bits + (plan.piece, cols))
-            own[chunk] = total
-            stage_refs[0][chunk] = total.astype(BF16)
-            launch(chunk, 0)
+            launch(chunk, 0, total.reshape((2,) * plan.bits + (plan.piece, cols)))
         else:
             ref, columns = target(chunk)
             ref[:, columns] = total
 
     if plan.scatter:
-        kept = {}
-        levels = len(plan.orders[0])
-        for stage in range(levels):
-            land = stage_refs[3 * stage + 1]
+        for stage in range(max(len(order) for order in plan.orders)):
             for chunk in range(plan.chunks):
+                if stage >= len(plan.orders[chunk]):
+                    continue
+                keep, _, land = refs[chunk, stage]
                 group = plan.orders[chunk][stage]
-                left = [b for b in reversed(range(plan.bits)) if b not in sum(plan.orders[chunk][:stage], ())]
-                where = tuple(bit_of[b] if b in group else slice(None) for b in left)
-                total = own[(chunk,) + where] if stage == 0 else kept[chunk].at_own(where)
+                where = tuple(
+                    bit_of[b] if b in group else slice(None) for b in plan.left(chunk, stage)
+                )
+                total = keep[where]
                 for place, copy in enumerate(flights[chunk, stage]):
                     copy.wait_recv()
-                    total = total + land[chunk, place].astype(F32)
-                if stage == levels - 1:
+                    total = total + land[place].astype(F32)
+                if stage == len(plan.orders[chunk]) - 1:
                     ref, columns = target(chunk)
                     ref[:, columns] = total
                 else:
-                    own_next = stage_refs[-1]
-                    own_next[chunk] = total
-                    stage_refs[3 * (stage + 1)][chunk] = total.astype(BF16)
-                    kept[chunk] = Kept(own_next, chunk)
-                    launch(chunk, stage + 1)
+                    launch(chunk, stage + 1, total)
 
     for copy in waiting:
         copy.wait_send()
-    for chunk in given.values() if not plan.scatter else ():
-        pass
     for copy in back_copies:
         copy.wait()
-
-
-class Kept:
-    def __init__(self, ref, chunk):
-        self.ref, self.chunk = ref, chunk
-
-    def at_own(self, where):
-        return self.ref[(self.chunk,) + where]
 
 
 def per_device(
@@ -359,6 +397,16 @@
     vmem = pltpu.VMEM
     dma = pltpu.SemaphoreType.DMA
     scratch = [
+        vmem((half, lat), F32),
+        vmem((half, lat), F32),
+        pltpu.SMEM(obs_count.shape, obs_count.dtype),
+        vmem(step_index.shape, step_index.dtype),
+        pltpu.SMEM(step_table.shape, F32),
+        vmem((lat, hl), BF16),
+        vmem((1, hl), F32),
+        vmem((lat, hl), BF16),
+        vmem((1, lat), F32),
+        dma((9,)),
         vmem((others, lat, hl), BF16),
         vmem((others, lat, hl), BF16),
         vmem((others, 1, hl), F32),
@@ -372,28 +420,23 @@
         vmem((sections, lat, half), BF16),
         vmem((others, plan.chunks, lat, plan.cols), BF16),
         vmem((others, plan.chunks, lat, plan.cols), BF16),
-        vmem(
-            (plan.chunks,) + ((2,) * plan.bits + (plan.piece, plan.cols) if plan.scatter else (8, 128)),
-            F32,
-        ),
         dma((2, others, 3)),
         dma((2, others, plan.chunks)),
         dma((2, others)),
     ]
     grad_rows = plan.piece if plan.scatter else lat
     if plan.scatter:
-        left = plan.bits
-        for group_size in [len(group) for group in plan.orders[0]]:
-            tail = (plan.piece, plan.cols)
-            masks = (1 << group_size) - 1
-            scratch.append(vmem((plan.chunks,) + (2,) * left + tail, BF16))
-            left -= group_size
-            scratch.append(vmem((plan.chunks, masks) + (2,) * left + tail, BF16))
-            scratch.append(dma((2, plan.chunks, masks)))
-        middle = plan.bits - len(plan.orders[0][0])
-        scratch.append(vmem((plan.chunks,) + (2,) * middle + (plan.piece, plan.cols), F32))
+        scratch.append(dma((2, plan.messages)))
+        tail = (plan.piece, plan.cols)
+        for chunk in range(plan.chunks):
+            for stage, group in enumerate(plan.orders[chunk]):
+                here = (2,) * len(plan.left(chunk, stage)) + tail
+                after = (2,) * len(plan.left(chunk, stage + 1)) + tail
+                scratch.append(vmem(here, F32))
+                scratch.append(vmem(here, BF16))
+                scratch.append(vmem(((1 << len(group)) - 1,) + after, BF16))
     in_vmem = pl.BlockSpec(memory_space=pltpu.VMEM)
-    in_smem = pl.BlockSpec(memory_space=pltpu.SMEM)
+    anywhere = pl.BlockSpec(memory_space=pl.ANY)
     back, grad_in, grad_out = pl.pallas_call(
         functools.partial(kernel, plan),
         name="adjoint",
@@ -402,7 +445,7 @@
             jax.ShapeDtypeStruct((grad_rows, hl), F32),
             jax.ShapeDtypeStruct((grad_rows, hl), F32),
         ),
-        in_specs=[in_vmem, in_vmem, in_smem, in_vmem, in_smem] + [in_vmem] * 4,
+        in_specs=[anywhere] * 9,
         out_specs=(in_vmem,) * 3,
         scratch_shapes=scratch,
         compiler_params=pltpu.CompilerParams(

time: 46.2 us -> 36.8 us (0.80)
  Pallas kernels: 41 us -> 31.6 us
    pallas_call x1, Pallas kernels: 41 us -> 31.6 us  [per_device(): pl.pallas_call(functools.partial(kernel, plan), name='adjoint', out_shape...]
where the time goes in v2:
time: 36.8 us; the launch traced here: 36.5 us
  Pallas kernels  31.6 us (86%)
  local copies, waits for them, and re-layouts  2.96 us (8%)
  other arithmetic  1.28 us (3%)
  between operations  0.65 us (2%)
    pallas_call x1, Pallas kernels, per_device(): pl.pallas_call(functools.partial(kernel, plan), name='adjoint', out_shape...  31.6 us
    unnamed x7, local copies, waits for them, and re-layouts  2.96 us
    broadcast_in_dim x1, other arithmetic, per_device(): b_hid.astype(F32)[None, :]  1.28 us

profile of v2, /device:TPU:0, one launch (start us, length us, event | category | flops | bytes accessed | tf_op | source)
XLA Modules:
  0.0 36.5 jit_solution(15672102184004047194)
XLA Ops:
  0.6 1.3 %broadcast_in_dim.11 = f32[1024]{0:T(1024)} convert(bf16[1024]{0:T(1024)(128)(2,1)} %param.15) | non-fusion elementwise | flops 1024 | bytes 6144 | tf_op jit(solution)/shard_map/broadcast_in_dim | solution.py:463
  1.9 31.6 %adjoint.1 = (f32[256,128]{1,0:T(8,128)}, f32[8,1024]{1,0:T(8,128)}, f32[8,1024]{1,0:T(8,128)}) custom-call(f32[256,128]{1,0:T(8,128)} %states_h.1, f32[256,128]{1,0:T(8,128)} %cotangent_h.1, s32[2]{0:T(128)} %obs_count_h.1, s32[2,256]{1,0:T(2,128)} %step_index_h.1, f32[16]{0:T(128)} %step_table_h.1, bf16[128,1024]{1,0:T(8,128)(2,1)} %w_in_h.1, ...), custom_call_target="tpu_custom_call" | custom-call | tf_op jit(solution)/shard_map/adjoint/pallas_call | solution.py:440
  33.5 0.0 copy-start.1
  33.5 1.6 %copy.15 = f32[256,128]{1,0:T(8,128)} copy(f32[256,128]{1,0:T(8,128)} %get-tuple-element.6) | data formatting | bytes 262144
  35.1 0.0 copy-done.1
  35.1 0.0 copy-start
  35.1 0.6 %copy.16 = f32[8,1024]{1,0:T(8,128)} copy(f32[8,1024]{1,0:T(8,128)S(1)} %copy-done.1) | data formatting | bytes 65536
  35.7 0.2 copy-done
  35.9 0.6 %copy.17 = f32[8,1024]{1,0:T(8,128)} copy(f32[8,1024]{1,0:T(8,128)S(1)} %copy-done) | data formatting | bytes 65536
Async XLA Ops:
  33.5 1.6 %copy-start.1 = (f32[8,1024]{1,0:T(8,128)S(1)}, f32[8,1024]{1,0:T(8,128)}, u32[]{:S(2)}) copy-start(f32[8,1024]{1,0:T(8,128)} %get-tuple-element.7) | copy-start | bytes 98308
  35.1 0.8 %copy-start = (f32[8,1024]{1,0:T(8,128)S(1)}, f32[8,1024]{1,0:T(8,128)}, u32[]{:S(2)}) copy-start(f32[8,1024]{1,0:T(8,128)} %get-tuple-element.8) | copy-start | bytes 98308

commit v3 on v2

--- a/solution.py
+++ b/solution.py
@@ -110,11 +110,11 @@
     (
         states, cotangent, obs_count, step_index, step_table, w_in, b_hid, w_out, b_out,
         local_sems,
-        win, wout, bias, win_t, wout_t, sizes, hid, hid_b, inner_b, vb_t, gb_t,
+        win, wout, bias, bias_rows, win_t, wout_t, sizes, hid, hid_b, inner_b, vb_t, gb_t,
         give, take,
         weight_sems, give_sems, back_sems,
-    ) = rest[3:29]
-    stage_refs = rest[29:]
+    ) = rest[3:30]
+    stage_refs = rest[30:]
     if plan.scatter:
         seq_sems = stage_refs[0]
         stage_refs = stage_refs[1:]
@@ -174,7 +174,7 @@
                 made.append(
                     pltpu.make_async_remote_copy(
                         src_ref=src,
-                        dst_ref=dst.at[n_par - k - 1],
+                        dst_ref=dst if len(dst.shape) == 1 else dst.at[n_par - k - 1],
                         send_sem=weight_sems.at[0, k - 1, which],
                         recv_sem=weight_sems.at[1, n_par - k - 1, which],
                         device_id={"par": peers[k]},
@@ -213,6 +213,11 @@
     for k in range(1, n_par):
         transposed(k, win.at[k - 1], wout.at[k - 1])
 
+    bias_rows[0:1, :] = b_hid[...].astype(F32).reshape(1, hl)
+    for k in range(1, n_par):
+        far = bias[...] if len(bias.shape) == 1 else bias[k - 1]
+        bias_rows[k : k + 1, :] = far.astype(F32).reshape(1, hl)
+
     def pieces():
         for k in range(n_par):
             for c in range(0, hl, plan.field_cols):
@@ -227,7 +232,7 @@
         return w_out[:, here] if k == 0 else wout[k - 1, :, here]
 
     def bias_at(k, here):
-        return b_hid[:, here] if k == 0 else bias[k - 1, :, here]
+        return bias_rows[k : k + 1, here]
 
     def forward(step, value):
         size = sizes[step]
@@ -242,7 +247,7 @@
             slope = jnp.broadcast_to(b_out[...], (half, plan.lat))
             for k, here, there in pieces():
                 hidden = jnp.tanh(dot(state_b, w_in_at(k, here)) + bias_at(k, here))
-                hid[at, :, there] = 1.0 - hidden * hidden
+                hid[at, :, there] = hidden
                 hid_b[at, :, there] = hidden.astype(BF16)
             slope = slope + dot(hid_b[at], wout_t[...])
             slopes.append(slope)
@@ -263,7 +268,7 @@
             grad_b = (size * weighted(coefs, [back] + adjoints[current + 1 :])).astype(BF16)
             gb_t[at] = grad_b.T
             for k, here, there in pieces():
-                inner = dot(grad_b, w_out_at(k, here)) * hid[at, :, there]
+                inner = dot(grad_b, w_out_at(k, here)) * (1.0 - hid[at, :, there] * hid[at, :, there])
                 inner_b[at, :, there] = inner.astype(BF16)
             adjoint = dot(inner_b[at], win_t[...])
             adjoints[current] = adjoint
@@ -282,8 +287,9 @@
 
     waiting = []
     given = {}
-    for k in range(1, n_par):
-        for chunk in range(plan.chunks):
+
+    def hand_over(chunk):
+        for k in range(1, n_par):
             give[k - 1, chunk] = gradient(k, chunk).astype(BF16)
             copy = pltpu.make_async_remote_copy(
                 src_ref=give.at[k - 1, chunk],
@@ -348,7 +354,10 @@
             flights[chunk, stage].append(copy)
             waiting.append(copy)
 
+    hand_over(0)
     for chunk in range(plan.chunks):
+        if chunk + 1 < plan.chunks:
+            hand_over(chunk + 1)
         total = gradient(0, chunk)
         for k in range(1, n_par):
             given[k - 1, chunk].wait_recv()
@@ -403,13 +412,14 @@
         vmem(step_index.shape, step_index.dtype),
         pltpu.SMEM(step_table.shape, F32),
         vmem((lat, hl), BF16),
-        vmem((1, hl), F32),
+        vmem((hl,), BF16),
         vmem((lat, hl), BF16),
         vmem((1, lat), F32),
         dma((9,)),
         vmem((others, lat, hl), BF16),
         vmem((others, lat, hl), BF16),
-        vmem((others, 1, hl), F32),
+        vmem((others, hl), BF16) if n_par > 2 else vmem((hl,), BF16),
+        vmem((n_par, hl), F32),
         vmem((hidden, lat), BF16),
         vmem((hidden, lat), BF16),
         vmem((STEPS, half, lat), F32),
@@ -460,7 +470,7 @@
         step_index,
         step_table,
         w_in,
-        b_hid.astype(F32)[None, :],
+        b_hid,
         w_out,
         b_out[None, :],
     )

time: 36.8 us -> 35 us (0.951)
  other arithmetic: 1.28 us -> 0 us
  Pallas kernels: 31.6 us -> 31.1 us
    broadcast_in_dim x1 -> x0, other arithmetic: 1.28 us -> none  [per_device(): b_hid.astype(F32)[None, :]]
    pallas_call x1, Pallas kernels: 31.6 us -> 31.1 us  [per_device(): pl.pallas_call(functools.partial(kernel, plan), name='adjoint', out_shape...]
where the time goes in v3:
time: 35 us; the launch traced here: 34.8 us
  Pallas kernels  31.1 us (89%)
  local copies, waits for them, and re-layouts  2.96 us (8%)
  between operations  0.65 us (2%)
    pallas_call x1, Pallas kernels, per_device(): pl.pallas_call(functools.partial(kernel, plan), name='adjoint', out_shape...  31.1 us
    unnamed x7, local copies, waits for them, and re-layouts  2.96 us

profile of v3, /device:TPU:0, one launch (start us, length us, event | category | flops | bytes accessed | tf_op | source)
XLA Modules:
  0.0 34.8 jit_solution(12600068367726592483)
XLA Ops:
  0.6 31.1 %adjoint.1 = (f32[256,128]{1,0:T(8,128)}, f32[8,1024]{1,0:T(8,128)}, f32[8,1024]{1,0:T(8,128)}) custom-call(f32[256,128]{1,0:T(8,128)} %states_h.1, f32[256,128]{1,0:T(8,128)} %cotangent_h.1, s32[2]{0:T(128)} %obs_count_h.1, s32[2,256]{1,0:T(2,128)} %step_index_h.1, f32[16]{0:T(128)} %step_table_h.1, bf16[128,1024]{1,0:T(8,128)(2,1)} %w_in_h.1, ...), custom_call_target="tpu_custom_call" | custom-call | tf_op jit(solution)/shard_map/adjoint/pallas_call | solution.py:450
  31.8 0.0 copy-start.1
  31.8 1.6 %copy.15 = f32[256,128]{1,0:T(8,128)} copy(f32[256,128]{1,0:T(8,128)} %get-tuple-element.6) | data formatting | bytes 262144
  33.4 0.0 copy-done.1
  33.4 0.0 copy-start
  33.4 0.6 %copy.16 = f32[8,1024]{1,0:T(8,128)} copy(f32[8,1024]{1,0:T(8,128)S(1)} %copy-done.1) | data formatting | bytes 65536
  34.0 0.2 copy-done
  34.1 0.6 %copy.17 = f32[8,1024]{1,0:T(8,128)} copy(f32[8,1024]{1,0:T(8,128)S(1)} %copy-done) | data formatting | bytes 65536
Async XLA Ops:
  31.8 1.6 %copy-start.1 = (f32[8,1024]{1,0:T(8,128)S(1)}, f32[8,1024]{1,0:T(8,128)}, u32[]{:S(2)}) copy-start(f32[8,1024]{1,0:T(8,128)} %get-tuple-element.7) | copy-start | bytes 98308
  33.4 0.8 %copy-start = (f32[8,1024]{1,0:T(8,128)S(1)}, f32[8,1024]{1,0:T(8,128)}, u32[]{:S(2)}) copy-start(f32[8,1024]{1,0:T(8,128)} %get-tuple-element.8) | copy-start | bytes 98308
